TPU v7x, 256 devices: a whole 4x4x8 slice. The times are simulated.
256 devices in a mesh: blk: 128 (over y, z, x_hi, core), mp: 2 (over x_lo).
Axes of the slice: x: 4 (x_hi: 2, x_lo: 2; x = x_hi * 2 + x_lo), y: 4, z: 8, core: 2. Of those that a mesh axis runs over, the one named last changes fastest.
Arguments:
- params: bfloat16 [128, 1024, 4096], P('blk', None, 'mp'), may hold values from -0.09375 to 0.09375
- hidden: bfloat16 [128, 384, 4096], P('blk', None, 'mp'), may hold values from -6 to 6
- targets: bfloat16 [128, 384, 1024], P('blk', None, 'mp'), may hold values from -6 to 6
Outputs:
- params_out: bfloat16 [128, 1024, 4096], P('blk', None, 'mp')
- errors: float32 [2], replicated
All inputs are finite; a program needn't handle non-finite values.
Results may differ from a plain program's by a relative error of at most 0.0085.
Values may be sent and summed in bfloat16 or wider, within the bound.
A program may use at most 128 MiB of HBM per device.

v0:
```python
import functools
import jax
import jax.numpy as jnp
from jax import lax
from jax.sharding import Mesh
from jax.sharding import PartitionSpec as P

ITERS = 2
BLK = ("blk_0", "blk_1", "blk_2", "blk_3")
BLK_MP = ("blk_0", "blk_1", "blk_2", "blk_3", "mp")
mix_third = 1.0 / 3.0
step_size = 0.1


def from_behind(block, axis, distance):
    devices = range(lax.axis_size(axis))
    route = [((i - distance) % len(devices), i) for i in devices]
    return lax.ppermute(block, axis, route)


def from_everyone(x, axis):
    copies = jnp.broadcast_to(x, (lax.axis_size(axis), *x.shape))
    return lax.all_to_all(copies, axis, split_axis=0, concat_axis=0, tiled=True)


def taken_together(x, axis):
    return from_everyone(x, axis).sum(axis=0)


def over_axes(x, axes):
    return functools.reduce(lax.psum, axes, x)


def send_tracker(track):
    track_left = from_behind(track, BLK, 1)
    track_right = from_behind(track, BLK, -1)
    return (track_left, track_right)


def on_device(params, hidden, targets):
    state = params[0]
    feats = hidden[0]
    targ_local = targets[0]
    tokens = feats.shape[0]
    hidden_total = state.shape[1] * lax.axis_size("mp")
    replicas = lax.axis_size(BLK)
    full_targ = lax.all_gather(targ_local, "mp", axis=1, tiled=True)

    def gradient(weight):
        partial_value = lax.dot_general(
            feats, weight, (((1,), (1,)), ((), ())), preferred_element_type=jnp.float32
        )
        output = taken_together(partial_value, "mp")
        resid = (output - full_targ.astype(jnp.float32)).astype(jnp.bfloat16)
        grad = lax.dot_general(
            resid, feats, (((0,), (0,)), ((), ())), preferred_element_type=jnp.float32
        )
        return grad / tokens

    older = gradient(state)
    fresh = older
    track = older.astype(jnp.bfloat16)
    track_left, track_right = send_tracker(track)
    err_list = []
    for step in range(ITERS):
        state_left = from_behind(state, BLK, 1)
        state_right = from_behind(state, BLK, -1)
        if step > 0:
            track_mix = (
                track_left.astype(jnp.float32)
                + track.astype(jnp.float32)
                + track_right.astype(jnp.float32)
            ) * mix_third
            track = (track_mix + fresh - older).astype(jnp.bfloat16)
            older = fresh
        own_state = state.astype(jnp.float32)
        diff = own_state - state_right.astype(jnp.float32)
        local_err = jnp.sum(diff * diff) / (hidden_total * replicas)
        err_list.append(local_err)
        blended = (
            state_left.astype(jnp.float32) + own_state + state_right.astype(jnp.float32)
        ) * mix_third
        new_state = (blended - step_size * track.astype(jnp.float32)).astype(jnp.bfloat16)
        if step < ITERS - 1:
            fresh = gradient(new_state)
        state = new_state
    errors = jnp.stack(err_list)
    errors = over_axes(errors, BLK_MP)
    return (state[None], errors)


def solution(mesh):
    torus = Mesh(
        mesh.devices.reshape(4, 8, 2, 2, mesh.shape["mp"]),
        ("blk_0", "blk_1", "blk_2", "blk_3", "mp"),
    )
    placed = (P(BLK, None, "mp"), P(BLK, None, "mp"), P(BLK, None, "mp"))
    return jax.shard_map(
        on_device, mesh=torus, in_specs=placed, out_specs=(P(BLK, None, "mp"), P()), check_vma=False
    )
```

profile of v0, /device:TPU:194, one launch (start us, length us, event | category | flops | bytes accessed | tf_op | source)
XLA Modules:
  0.0 420.3 jit_solution(9891182136154639013)
XLA Ops:
  0.6 0.0 copy-start
  0.6 2.1 collective-permute-start.1
  2.7 0.0 collective-permute-start
  2.7 0.0 copy-done
  2.7 4.0 fusion.23
  6.8 2.1 broadcast_in_dim.9
  8.8 0.0 copy-start.2
  8.8 6.8 %all-to-all-start = ((f32[2,384,1024]{2,1,0:T(8,128)}), f32[2,384,1024]{2,1,0:T(8,128)}, u32[]{:S(2)}, u32[]{:S(2)}) async-start(f32[2,384,1024]{2,1,0:T(8,128)} %broadcast_in_dim.9), calls=%async_computation | async-start | bytes 6291456 | tf_op jit(solution)/shard_map/all_to_all | solution.py:23
  15.6 0.0 copy-done.2
  15.6 78.1 %all-gather = bf16[1,384,1024]{2,1,0:T(8,128)(2,1)} all-gather(bf16[1,384,512]{2,1,0:T(8,128)(2,1)S(1)} %copy-done.2), channel_id=2, replica_groups=mesh['blk_0'=4,'blk_1'=8,'blk_2'=2,'blk_3'=2,'mp'=2] {'mp'}, dimensions={2}, use_global_device_ids=true | all-gather | bytes 1179648 | tf_op jit(solution)/shard_map/all_gather | solution.py:47
  93.6 0.0 all-to-all-done
  93.6 2.3 reduce_sum.36
  96.0 0.0 collective-permute-done.1
  96.0 0.0 collective-permute-done
  96.0 13.7 %fusion.4 = (f32[]{:T(128)}, bf16[1024,2048]{1,0:T(8,128)(2,1)}, bf16[1024,2048]{1,0:T(8,128)(2,1)}, f32[1024,2048]{1,0:T(8,128)}) fusion(bf16[1024,2048]{1,0:T(8,128)(2,1)} %collective-permute-done.1, bf16[1,1024,2048]{2,1,0:T(8,128)(2,1)} %param.3, bf16[1024,2048]{1,0:T(8,128)(2,1)} %collective-permute-done, bf16[1,384,2048]{2,1,0:T(8,128)(2,1)S(1)} %copy-done, ...), kind=kOutput, calls=%fused_computation.12 | convolution fusion | flops 1643249664 | bytes 33292292 | tf_op jit(solution)/shard_map/dot_general | solution.py:55
  109.7 3.0 collective-permute-start.3
  112.7 86.1 %collective-permute-start.4 = (bf16[1024,2048]{1,0:T(8,128)(2,1)}, bf16[1024,2048]{1,0:T(8,128)(2,1)}, u32[]{:S(2)}, u32[]{:S(2)}) collective-permute-start(bf16[1024,2048]{1,0:T(8,128)(2,1)} %get-tuple-element.4), channel_id=1, source_target_pairs={{254,0},{0,2},{2,4},{4,6},{6,8},{8,10},{10,12},{12,14},{14,16},{16... | collective-permute-start | bytes 12582920 | tf_op jit(solution)/shard_map/ppermute | solution.py:18
  198.8 0.0 collective-permute-start.5
  198.8 3.2 collective-permute-start.2
  202.1 4.0 fusion.25
  206.1 2.1 broadcast_in_dim.10
  208.2 6.6 %all-to-all-start.1 = ((f32[2,384,1024]{2,1,0:T(8,128)}), f32[2,384,1024]{2,1,0:T(8,128)}, u32[]{:S(2)}, u32[]{:S(2)}) async-start(f32[2,384,1024]{2,1,0:T(8,128)} %broadcast_in_dim.10), calls=%async_computation.1 | async-start | bytes 6291456 | tf_op jit(solution)/shard_map/all_to_all | solution.py:23
  215.4 0.0 collective-permute-done.3
  215.4 6.3 %fusion.14 = f32[]{:T(128)} fusion(bf16[1024,2048]{1,0:T(8,128)(2,1)} %collective-permute-done.3, bf16[1024,2048]{1,0:T(8,128)(2,1)} %get-tuple-element.3), kind=kLoop, calls=%fused_computation.22 | loop fusion | flops 10485759 | bytes 8388612 | tf_op jit(solution)/shard_map/reduce_sum | solution.py:78
  221.7 0.0 copy-start.1
  222.4 0.1 pad_maximum_fusion
  222.5 10.7 %psum.35 = f32[2]{0:T(128)S(1)} all-reduce(f32[2]{0:T(128)S(1)} %pad_maximum_fusion), channel_id=1, replica_groups=mesh['blk_0'=4,'blk_1'=8,'blk_2'=2,'blk_3'=2,'mp'=2] {'blk_0'}, use_global_device_ids=true, to_apply=%region_4.0 | all-reduce | flops 2 | bytes 16 | tf_op jit(solution)/shard_map/psum | solution.py:31
  233.2 22.5 %psum.36 = f32[2]{0:T(128)S(1)} all-reduce(f32[2]{0:T(128)S(1)} %psum.35), channel_id=1, replica_groups=mesh['blk_0'=4,'blk_1'=8,'blk_2'=2,'blk_3'=2,'mp'=2] {'blk_1'}, use_global_device_ids=true, to_apply=%region_5.0 | all-reduce | flops 2 | bytes 16 | tf_op jit(solution)/shard_map/psum | solution.py:31
  255.7 138.1 %psum.37 = f32[2]{0:T(128)S(1)} all-reduce(f32[2]{0:T(128)S(1)} %psum.36), channel_id=1, replica_groups=mesh['blk_0'=4,'blk_1'=8,'blk_2'=2,'blk_3'=2,'mp'=2] {'blk_2'}, use_global_device_ids=true, to_apply=%region_6.0 | all-reduce | flops 2 | bytes 16 | tf_op jit(solution)/shard_map/psum | solution.py:31
  393.7 2.4 psum.38
  396.2 0.0 all-to-all-done.1
  396.2 3.5 reduce_sum.37
  399.6 5.4 %psum.39 = f32[2]{0:T(128)} all-reduce(f32[2]{0:T(128)S(1)} %psum.38), channel_id=1, replica_groups=mesh['blk_0'=4,'blk_1'=8,'blk_2'=2,'blk_3'=2,'mp'=2] {'mp'}, use_global_device_ids=true, to_apply=%region_8.0 | all-reduce | flops 2 | bytes 16 | tf_op jit(solution)/shard_map/psum | solution.py:31
  405.1 0.0 collective-permute-done.4
  405.1 0.0 collective-permute-done.5
  405.1 0.0 collective-permute-done.2
  405.1 0.0 copy-done.1
  405.1 15.3 %fusion.15 = bf16[1,1024,2048]{2,1,0:T(8,128)(2,1)} fusion(bf16[1024,2048]{1,0:T(8,128)(2,1)} %collective-permute-done.3, bf16[1024,2048]{1,0:T(8,128)(2,1)} %get-tuple-element.3, bf16[1024,2048]{1,0:T(8,128)(2,1)} %collective-permute-done.2, f32[1024,2048]{1,0:T(8,128)} %get-tuple-element.5, bf16[1024,2048]{1,0:T(8,128)(2,1)} %collective-permute-done.5, ...), kind=kOutput, calls=%fused_computation.24 | convolution fusion | flops 1657929728 | bytes 37486592 | tf_op jit(solution)/shard_map/dot_general | solution.py:55
Async XLA Ops:
  0.6 2.1 copy-start
  0.6 95.3 %collective-permute-start.1 = (bf16[1024,2048]{1,0:T(8,128)(2,1)}, bf16[1024,2048]{1,0:T(8,128)(2,1)}, u32[]{:S(2)}, u32[]{:S(2)}) collective-permute-start(bf16[1024,2048]{1,0:T(8,128)(2,1)} %bitcast.37), channel_id=1, source_target_pairs={{2,0},{4,2},{6,4},{8,6},{10,8},{12,10},{14,12},{16,14},{18,16},{20... | collective-permute-start | bytes 12582920 | tf_op jit(solution)/shard_map/ppermute | solution.py:18
  2.7 93.2 %collective-permute-start = (bf16[1024,2048]{1,0:T(8,128)(2,1)}, bf16[1024,2048]{1,0:T(8,128)(2,1)}, u32[]{:S(2)}, u32[]{:S(2)}) collective-permute-start(bf16[1024,2048]{1,0:T(8,128)(2,1)} %bitcast.38), channel_id=1, source_target_pairs={{254,0},{0,2},{2,4},{4,6},{6,8},{8,10},{10,12},{12,14},{14,16},{16... | collective-permute-start | bytes 12582920 | tf_op jit(solution)/shard_map/ppermute | solution.py:18
  8.8 6.8 %copy-start.2 = (bf16[1,384,512]{2,1,0:T(8,128)(2,1)S(1)}, bf16[1,384,512]{2,1,0:T(8,128)(2,1)}, u32[]{:S(2)}) copy-start(bf16[1,384,512]{2,1,0:T(8,128)(2,1)} %param.5) | copy-start | bytes 1179652
  8.8 84.8 %all-to-all-start = ((f32[2,384,1024]{2,1,0:T(8,128)}), f32[2,384,1024]{2,1,0:T(8,128)}, u32[]{:S(2)}, u32[]{:S(2)}) async-start(f32[2,384,1024]{2,1,0:T(8,128)} %broadcast_in_dim.9), calls=%async_computation | async-start | bytes 6291456 | tf_op jit(solution)/shard_map/all_to_all | solution.py:23
  109.7 105.7 %collective-permute-start.3 = (bf16[1024,2048]{1,0:T(8,128)(2,1)}, bf16[1024,2048]{1,0:T(8,128)(2,1)}, u32[]{:S(2)}, u32[]{:S(2)}) collective-permute-start(bf16[1024,2048]{1,0:T(8,128)(2,1)} %get-tuple-element.3), channel_id=1, source_target_pairs={{2,0},{4,2},{6,4},{8,6},{10,8},{12,10},{14,12},{16,14},{18,16},{20... | collective-permute-start | bytes 12582920 | tf_op jit(solution)/shard_map/ppermute | solution.py:18
  112.7 292.4 %collective-permute-start.4 = (bf16[1024,2048]{1,0:T(8,128)(2,1)}, bf16[1024,2048]{1,0:T(8,128)(2,1)}, u32[]{:S(2)}, u32[]{:S(2)}) collective-permute-start(bf16[1024,2048]{1,0:T(8,128)(2,1)} %get-tuple-element.4), channel_id=1, source_target_pairs={{254,0},{0,2},{2,4},{4,6},{6,8},{8,10},{10,12},{12,14},{14,16},{16... | collective-permute-start | bytes 12582920 | tf_op jit(solution)/shard_map/ppermute | solution.py:18
  198.8 206.2 %collective-permute-start.5 = (bf16[1024,2048]{1,0:T(8,128)(2,1)}, bf16[1024,2048]{1,0:T(8,128)(2,1)}, u32[]{:S(2)}, u32[]{:S(2)}) collective-permute-start(bf16[1024,2048]{1,0:T(8,128)(2,1)} %get-tuple-element.4), channel_id=1, source_target_pairs={{2,0},{4,2},{6,4},{8,6},{10,8},{12,10},{14,12},{16,14},{18,16},{20... | collective-permute-start | bytes 12582920 | tf_op jit(solution)/shard_map/ppermute | solution.py:18
  198.8 206.2 %collective-permute-start.2 = (bf16[1024,2048]{1,0:T(8,128)(2,1)}, bf16[1024,2048]{1,0:T(8,128)(2,1)}, u32[]{:S(2)}, u32[]{:S(2)}) collective-permute-start(bf16[1024,2048]{1,0:T(8,128)(2,1)} %get-tuple-element.3), channel_id=1, source_target_pairs={{254,0},{0,2},{2,4},{4,6},{6,8},{8,10},{10,12},{12,14},{14,16},{16... | collective-permute-start | bytes 12582920 | tf_op jit(solution)/shard_map/ppermute | solution.py:18
  208.2 188.0 %all-to-all-start.1 = ((f32[2,384,1024]{2,1,0:T(8,128)}), f32[2,384,1024]{2,1,0:T(8,128)}, u32[]{:S(2)}, u32[]{:S(2)}) async-start(f32[2,384,1024]{2,1,0:T(8,128)} %broadcast_in_dim.10), calls=%async_computation.1 | async-start | bytes 6291456 | tf_op jit(solution)/shard_map/all_to_all | solution.py:23
  221.7 183.4 %copy-start.1 = (bf16[1,384,1024]{2,1,0:T(8,128)(2,1)S(1)}, bf16[1,384,1024]{2,1,0:T(8,128)(2,1)}, u32[]{:S(2)}) copy-start(bf16[1,384,1024]{2,1,0:T(8,128)(2,1)} %all-gather) | copy-start | bytes 2359300
where the time goes:
time: 421 us; the launch traced here: 420 us
  blocking collectives  257 us (61%)
  starting transfers between devices  108 us (26%)
  matrix products  37.1 us (9%)
  other arithmetic  12.1 us (3%)
    psum x5, blocking collectives, over_axes(): return functools.reduce(lax.psum, axes, x)  179 us
    ppermute x6, starting transfers between devices, from_behind(): return lax.ppermute(block, axis, route)  94.4 us
    all_gather x1, blocking collectives, on_device(): full_targ = lax.all_gather(targ_local, 'mp', axis=1, tiled=True)  78.1 us
    dot_general x2, matrix products, gradient(): lax.dot_general(resid, feats, (((0,), (0,)), ((), ())), preferred_element...  29 us
    all_to_all x2, starting transfers between devices, from_everyone(): return lax.all_to_all(copies, axis, split_axis=0, concat_axis=0, tiled=True)  13.3 us
  transfers between devices with their start and end apart: 8, of which 0 were waited for; matrix products, arithmetic and copies ran while one was open for 6% of the time, Pallas kernels for 0%

commit v1 on v0

--- a/solution.py
+++ b/solution.py
@@ -44,7 +44,8 @@
     tokens = feats.shape[0]
     hidden_total = state.shape[1] * lax.axis_size("mp")
     replicas = lax.axis_size(BLK)
-    full_targ = lax.all_gather(targ_local, "mp", axis=1, tiled=True)
+    play_ways = lambda work_x: jnp.concatenate(lax.all_gather(work_x, axis_name="mp"), axis=1)
+    full_targ = play_ways(targ_local)
 
     def gradient(weight):
         partial_value = lax.dot_general(

time: 421 us -> 416 us (0.988); the launches traced: 420 us -> 411 us
  blocking collectives: 257 us -> 208 us
  waiting for transfers between devices: 0.02 us -> 25.6 us
  local copies, waits for them, and re-layouts: 4.16 us -> 15.1 us
  other arithmetic: 12.1 us -> 16.4 us
    psum x5, blocking collectives: 179 us -> 130 us  [over_axes(): return functools.reduce(lax.psum, axes, x)]
    all_to_all x2, waiting for transfers between devices: 0.01 us -> 25.6 us  [from_everyone(): return lax.all_to_all(copies, axis, split_axis=0, concat_axis=0, tiled=True)]
    reduce_sum x0 -> x2, local copies, waits for them, and re-layouts: none -> 6.1 us  [taken_together(): return from_everyone(x, axis).sum(axis=0)]
  transfers between devices with their start and end apart: 8 -> 8, of which waited for: 0 -> 1; matrix products, arithmetic and copies ran while one was open for 6% -> 10% of each run, Pallas kernels for 0% -> 0%
where the time goes in v1:
time: 416 us; the launch traced here: 411 us
  blocking collectives  208 us (50%)
  starting transfers between devices  108 us (26%)
  matrix products  36.1 us (9%)
  waiting for transfers between devices  25.6 us (6%)
  other arithmetic  16.4 us (4%)
  local copies, waits for them, and re-layouts  15.1 us (4%)
    psum x5, blocking collectives, over_axes(): return functools.reduce(lax.psum, axes, x)  130 us
    ppermute x6, starting transfers between devices, from_behind(): return lax.ppermute(block, axis, route)  94.5 us
    all_gather x1, blocking collectives, on_device(): lax.all_gather(work_x, axis_name='mp')  77.9 us
    dot_general x2, matrix products, gradient(): lax.dot_general(resid, feats, (((0,), (0,)), ((), ())), preferred_element...  26.4 us
    all_to_all x2, waiting for transfers between devices, from_everyone(): return lax.all_to_all(copies, axis, split_axis=0, concat_axis=0, tiled=True)  25.6 us
    all_to_all x2, starting transfers between devices, from_everyone(): return lax.all_to_all(copies, axis, split_axis=0, concat_axis=0, tiled=True)  13.3 us
    dot_general x2, matrix products, gradient(): lax.dot_general(feats, weight, (((1,), (1,)), ((), ())), preferred_elemen...  9.7 us
  transfers between devices with their start and end apart: 8, of which 1 were waited for; matrix products, arithmetic and copies ran while one was open for 10% of the time, Pallas kernels for 0%

profile of v1, /device:TPU:194, one launch (start us, length us, event | category | flops | bytes accessed | tf_op | source)
XLA Modules:
  0.0 410.7 jit_solution(1578110732319820831)
XLA Ops:
  0.6 0.0 copy-start
  0.6 2.1 collective-permute-start.1
  2.7 0.0 collective-permute-start
  2.7 0.0 copy-done
  2.7 4.0 fusion.23
  6.8 2.1 broadcast_in_dim.9
  8.8 0.0 copy-start.1
  8.8 6.8 %all-to-all-start = ((f32[2,384,1024]{2,1,0:T(8,128)}), f32[2,384,1024]{2,1,0:T(8,128)}, u32[]{:S(2)}, u32[]{:S(2)}) async-start(f32[2,384,1024]{2,1,0:T(8,128)} %broadcast_in_dim.9), calls=%async_computation | async-start | bytes 6291456 | tf_op jit(solution)/shard_map/all_to_all | solution.py:23
  15.6 0.0 copy-done.1
  15.6 77.9 %all_gather.3 = bf16[2,384,512]{2,1,0:T(8,128)(2,1)S(1)} all-gather(bf16[1,384,512]{2,1,0:T(8,128)(2,1)S(1)} %copy-done.1), channel_id=1, replica_groups=mesh['blk_0'=4,'blk_1'=8,'blk_2'=2,'blk_3'=2,'mp'=2] {'mp'}, dimensions={0}, use_global_device_ids=true | all-gather | bytes 1179648 | tf_op jit(solution)/shard_map/all_gather | solution.py:47
  93.5 0.4 copy.11
  93.9 0.0 all-to-all-done
  93.9 3.5 reduce_sum.40
  97.4 3.0 copy.10
  100.4 1.6 fusion.16
  102.0 0.0 collective-permute-done.1
  102.0 0.0 collective-permute-done
  102.0 12.1 %fusion.4 = (f32[]{:T(128)}, bf16[1024,2048]{1,0:T(8,128)(2,1)}, bf16[1024,2048]{1,0:T(8,128)(2,1)}, f32[1024,2048]{1,0:T(8,128)}) fusion(bf16[1024,2048]{1,0:T(8,128)(2,1)} %collective-permute-done.1, bf16[1,1024,2048]{2,1,0:T(8,128)(2,1)} %param.3, bf16[1024,2048]{1,0:T(8,128)(2,1)} %collective-permute-done, bf16[384,1024]{0,1:T(8,128)(2,1)S(1)} %bitcast.42, ...), kind=kOutput, calls=%fused_computation.12 | convolution fusion | flops 1642070016 | bytes 31719428 | tf_op jit(solution)/shard_map/dot_general | solution.py:56
  114.1 3.1 collective-permute-start.3
  117.2 86.1 %collective-permute-start.4 = (bf16[1024,2048]{1,0:T(8,128)(2,1)}, bf16[1024,2048]{1,0:T(8,128)(2,1)}, u32[]{:S(2)}, u32[]{:S(2)}) collective-permute-start(bf16[1024,2048]{1,0:T(8,128)(2,1)} %get-tuple-element.4), channel_id=1, source_target_pairs={{254,0},{0,2},{2,4},{4,6},{6,8},{8,10},{10,12},{12,14},{14,16},{16... | collective-permute-start | bytes 12582920 | tf_op jit(solution)/shard_map/ppermute | solution.py:18
  203.3 0.0 collective-permute-start.5
  203.3 3.2 collective-permute-start.2
  206.5 5.7 %fusion.25 = f32[384,1024]{0,1:T(8,128)} fusion(bf16[1024,2048]{1,0:T(8,128)(2,1)} %get-tuple-element.3, bf16[1,384,2048]{2,1,0:T(8,128)(2,1)S(1)} %copy-done), kind=kOutput, calls=%fused_computation.36 | convolution fusion | flops 1610612736 | bytes 7340032 | tf_op jit(solution)/shard_map/dot_general | solution.py:51
  212.2 3.1 copy.12
  215.3 3.5 broadcast_in_dim.10
  218.8 6.6 %all-to-all-start.1 = ((f32[2,384,1024]{2,1,0:T(8,128)}), f32[2,384,1024]{2,1,0:T(8,128)}, u32[]{:S(2)}, u32[]{:S(2)}) async-start(f32[2,384,1024]{2,1,0:T(8,128)} %broadcast_in_dim.10), calls=%async_computation.1 | async-start | bytes 6291456 | tf_op jit(solution)/shard_map/all_to_all | solution.py:23
  226.0 0.0 collective-permute-done.3
  226.0 6.3 %fusion.14 = f32[]{:T(128)} fusion(bf16[1024,2048]{1,0:T(8,128)(2,1)} %collective-permute-done.3, bf16[1024,2048]{1,0:T(8,128)(2,1)} %get-tuple-element.3), kind=kLoop, calls=%fused_computation.22 | loop fusion | flops 10485759 | bytes 8388612 | tf_op jit(solution)/shard_map/reduce_sum | solution.py:79
  232.9 0.1 pad_maximum_fusion
  233.0 10.7 %psum.35 = f32[2]{0:T(128)S(1)} all-reduce(f32[2]{0:T(128)S(1)} %pad_maximum_fusion), channel_id=1, replica_groups=mesh['blk_0'=4,'blk_1'=8,'blk_2'=2,'blk_3'=2,'mp'=2] {'blk_0'}, use_global_device_ids=true, to_apply=%region_4.0 | all-reduce | flops 2 | bytes 16 | tf_op jit(solution)/shard_map/psum | solution.py:31
  243.7 16.4 %psum.36 = f32[2]{0:T(128)S(1)} all-reduce(f32[2]{0:T(128)S(1)} %psum.35), channel_id=1, replica_groups=mesh['blk_0'=4,'blk_1'=8,'blk_2'=2,'blk_3'=2,'mp'=2] {'blk_1'}, use_global_device_ids=true, to_apply=%region_5.0 | all-reduce | flops 2 | bytes 16 | tf_op jit(solution)/shard_map/psum | solution.py:31
  260.1 25.6 %all-to-all-done.1 = f32[2,384,1024]{2,1,0:T(8,128)} async-done(((f32[2,384,1024]{2,1,0:T(8,128)}), f32[2,384,1024]{2,1,0:T(8,128)}, u32[]{:S(2)}, u32[]{:S(2)}) %all-to-all-start.1) | async-done | bytes 3145760 | tf_op jit(solution)/shard_map/all_to_all | solution.py:23
  285.7 3.5 reduce_sum.42
  289.1 94.7 %psum.37 = f32[2]{0:T(128)S(1)} all-reduce(f32[2]{0:T(128)S(1)} %psum.36), channel_id=1, replica_groups=mesh['blk_0'=4,'blk_1'=8,'blk_2'=2,'blk_3'=2,'mp'=2] {'blk_2'}, use_global_device_ids=true, to_apply=%region_6.0 | all-reduce | flops 2 | bytes 16 | tf_op jit(solution)/shard_map/psum | solution.py:31
  383.9 3.1 copy.13
  387.0 2.4 psum.38
  389.4 1.6 fusion.17
  391.0 5.4 %psum.39 = f32[2]{0:T(128)} all-reduce(f32[2]{0:T(128)S(1)} %psum.38), channel_id=1, replica_groups=mesh['blk_0'=4,'blk_1'=8,'blk_2'=2,'blk_3'=2,'mp'=2] {'mp'}, use_global_device_ids=true, to_apply=%region_8.0 | all-reduce | flops 2 | bytes 16 | tf_op jit(solution)/shard_map/psum | solution.py:31
  396.4 0.0 collective-permute-done.4
  396.4 0.0 collective-permute-done.5
  396.4 0.0 collective-permute-done.2
  396.4 14.3 %fusion.15 = bf16[1,1024,2048]{2,1,0:T(8,128)(2,1)} fusion(bf16[1024,2048]{1,0:T(8,128)(2,1)} %collective-permute-done.3, bf16[1024,2048]{1,0:T(8,128)(2,1)} %get-tuple-element.3, bf16[1024,2048]{1,0:T(8,128)(2,1)} %collective-permute-done.2, f32[1024,2048]{1,0:T(8,128)} %get-tuple-element.5, bf16[384,1024]{0,1:T(8,128)(2,1)S(1)} %bitcast.43, ...), kind=kOutput, calls=%fused_computation.24 | convolution fusion | flops 1656750080 | bytes 35913728 | tf_op jit(solution)/shard_map/dot_general | solution.py:56
Async XLA Ops:
  0.6 2.1 copy-start
  0.6 101.3 %collective-permute-start.1 = (bf16[1024,2048]{1,0:T(8,128)(2,1)}, bf16[1024,2048]{1,0:T(8,128)(2,1)}, u32[]{:S(2)}, u32[]{:S(2)}) collective-permute-start(bf16[1024,2048]{1,0:T(8,128)(2,1)} %bitcast.40), channel_id=1, source_target_pairs={{2,0},{4,2},{6,4},{8,6},{10,8},{12,10},{14,12},{16,14},{18,16},{20... | collective-permute-start | bytes 12582920 | tf_op jit(solution)/shard_map/ppermute | solution.py:18
  2.7 99.2 %collective-permute-start = (bf16[1024,2048]{1,0:T(8,128)(2,1)}, bf16[1024,2048]{1,0:T(8,128)(2,1)}, u32[]{:S(2)}, u32[]{:S(2)}) collective-permute-start(bf16[1024,2048]{1,0:T(8,128)(2,1)} %bitcast.41), channel_id=1, source_target_pairs={{254,0},{0,2},{2,4},{4,6},{6,8},{8,10},{10,12},{12,14},{14,16},{16... | collective-permute-start | bytes 12582920 | tf_op jit(solution)/shard_map/ppermute | solution.py:18
  8.8 6.8 %copy-start.1 = (bf16[1,384,512]{2,1,0:T(8,128)(2,1)S(1)}, bf16[1,384,512]{2,1,0:T(8,128)(2,1)}, u32[]{:S(2)}) copy-start(bf16[1,384,512]{2,1,0:T(8,128)(2,1)} %param.5) | copy-start | bytes 1179652
  8.8 85.1 %all-to-all-start = ((f32[2,384,1024]{2,1,0:T(8,128)}), f32[2,384,1024]{2,1,0:T(8,128)}, u32[]{:S(2)}, u32[]{:S(2)}) async-start(f32[2,384,1024]{2,1,0:T(8,128)} %broadcast_in_dim.9), calls=%async_computation | async-start | bytes 6291456 | tf_op jit(solution)/shard_map/all_to_all | solution.py:23
  114.1 111.9 %collective-permute-start.3 = (bf16[1024,2048]{1,0:T(8,128)(2,1)}, bf16[1024,2048]{1,0:T(8,128)(2,1)}, u32[]{:S(2)}, u32[]{:S(2)}) collective-permute-start(bf16[1024,2048]{1,0:T(8,128)(2,1)} %get-tuple-element.3), channel_id=1, source_target_pairs={{2,0},{4,2},{6,4},{8,6},{10,8},{12,10},{14,12},{16,14},{18,16},{20... | collective-permute-start | bytes 12582920 | tf_op jit(solution)/shard_map/ppermute | solution.py:18
  117.2 279.3 %collective-permute-start.4 = (bf16[1024,2048]{1,0:T(8,128)(2,1)}, bf16[1024,2048]{1,0:T(8,128)(2,1)}, u32[]{:S(2)}, u32[]{:S(2)}) collective-permute-start(bf16[1024,2048]{1,0:T(8,128)(2,1)} %get-tuple-element.4), channel_id=1, source_target_pairs={{254,0},{0,2},{2,4},{4,6},{6,8},{8,10},{10,12},{12,14},{14,16},{16... | collective-permute-start | bytes 12582920 | tf_op jit(solution)/shard_map/ppermute | solution.py:18
  203.3 193.1 %collective-permute-start.5 = (bf16[1024,2048]{1,0:T(8,128)(2,1)}, bf16[1024,2048]{1,0:T(8,128)(2,1)}, u32[]{:S(2)}, u32[]{:S(2)}) collective-permute-start(bf16[1024,2048]{1,0:T(8,128)(2,1)} %get-tuple-element.4), channel_id=1, source_target_pairs={{2,0},{4,2},{6,4},{8,6},{10,8},{12,10},{14,12},{16,14},{18,16},{20... | collective-permute-start | bytes 12582920 | tf_op jit(solution)/shard_map/ppermute | solution.py:18
  203.3 193.1 %collective-permute-start.2 = (bf16[1024,2048]{1,0:T(8,128)(2,1)}, bf16[1024,2048]{1,0:T(8,128)(2,1)}, u32[]{:S(2)}, u32[]{:S(2)}) collective-permute-start(bf16[1024,2048]{1,0:T(8,128)(2,1)} %get-tuple-element.3), channel_id=1, source_target_pairs={{254,0},{0,2},{2,4},{4,6},{6,8},{8,10},{10,12},{12,14},{14,16},{16... | collective-permute-start | bytes 12582920 | tf_op jit(solution)/shard_map/ppermute | solution.py:18
  218.8 66.9 %all-to-all-start.1 = ((f32[2,384,1024]{2,1,0:T(8,128)}), f32[2,384,1024]{2,1,0:T(8,128)}, u32[]{:S(2)}, u32[]{:S(2)}) async-start(f32[2,384,1024]{2,1,0:T(8,128)} %broadcast_in_dim.10), calls=%async_computation.1 | async-start | bytes 6291456 | tf_op jit(solution)/shard_map/all_to_all | solution.py:23
